TPU v7x, 16 devices: a 4x2x1 block of a 4x4x8 slice. The times are simulated.
16 devices in a mesh: dp: 2 (over y, z), tp: 8 (over x, core).
Axes of the slice: x: 4, y: 2, z: 1, core: 2. Of those that a mesh axis runs over, the one named last changes fastest.
The devices are a block of a 4x4x8 slice.
Arguments:
- x: bfloat16 [4096, 4096], P(('dp', 'tp')), parts along dimension 0
- w_gate: bfloat16 [4096, 10240], P(None, 'tp')
- w_up: bfloat16 [4096, 10240], P(None, 'tp')
- w_down: bfloat16 [10240, 4096], P('tp')
Outputs:
- output: bfloat16 [4096, 4096], P(('dp', 'tp')), parts along dimension 0
There are 2 independent parts. A program takes and returns all parts, laid end to end along the dimension named above; an argument that names none is the same for every part.
All inputs are finite; a program needn't handle non-finite values.
Results may differ from a plain program's by a relative error of at most 0.016.
Values are sent between devices in bfloat16 or wider.
A program may use at most 768 MiB of HBM per device.

v0:
```python
import jax
import jax.numpy as jnp
from jax import lax
from jax.sharding import PartitionSpec as P


def solution(mesh):
    def step(x, w_gate, w_up, w_down):
        rows = lax.all_gather(x, "tp", axis=0, tiled=True)
        gate = jnp.dot(rows, w_gate, preferred_element_type=jnp.float32)
        up = jnp.dot(rows, w_up, preferred_element_type=jnp.float32)
        hidden = (jax.nn.gelu(gate) * up).astype(jnp.bfloat16)
        term = jnp.dot(hidden, w_down, preferred_element_type=jnp.float32).astype(jnp.bfloat16)
        return lax.psum_scatter(term, "tp", scatter_dimension=0, tiled=True)

    return jax.shard_map(
        step,
        mesh=mesh,
        in_specs=(P(("dp", "tp"), None), P(None, "tp"), P(None, "tp"), P("tp", None)),
        out_specs=P(("dp", "tp"), None),
        check_vma=False,
    )
```

profile of v0, /device:TPU:112, one launch (start us, length us, event | category | flops | bytes accessed | tf_op | source)
XLA Modules:
  0.0 274.4 jit_solution(16251043425955621931)
XLA Ops:
  6.5 0.0 all-gather.2.cloned.1.call-start
  6.6 0.7 all-gather.2.cloned.1.call-update
  7.3 0.1 reduce-scatter.2.cloned.1.call-start
  7.4 85.5 %all-gather.2.cloned.1.call-done = bf16[2048,4096]{1,0:T(8,128)(2,1)} async-done(((bf16[256,4096]{1,0:T(8,128)(2,1)}), bf16[2048,4096]{1,0:T(8,128)(2,1)}) %all-gather.2.cloned.1.call-update) | async-done | bytes 16777232 | tf_op jit(solution)/shard_map/all_gather | solution.py:9
  92.9 0.0 copy-start
  92.9 29.2 %fusion.13 = f32[2048,1280]{1,0:T(8,128)} fusion(bf16[2048,4096]{1,0:T(8,128)(2,1)} %all-gather.2.cloned.1.call-done, bf16[4096,1280]{1,0:T(8,128)(2,1)} %param.5), kind=kOutput, calls=%fused_computation.15 | convolution fusion | flops 21474836480 | bytes 37748736 | tf_op jit(solution)/shard_map/dot_general | solution.py:10
  122.2 0.0 copy-done
  122.2 29.6 %fusion.8.clone.4 = bf16[2048,1280]{1,0:T(8,128)(2,1)S(1)} fusion(f32[2048,1280]{1,0:T(8,128)} %fusion.13, bf16[2048,4096]{1,0:T(8,128)(2,1)S(1)} %copy-done, bf16[4096,1280]{1,0:T(8,128)(2,1)} %param.6), kind=kOutput, calls=%fused_computation.10.clone.clone.clone.1 | convolution fusion | flops 21501050880 | bytes 42991616 | tf_op jit(solution)/shard_map/dot_general | solution.py:11
  151.8 27.2 %convolution_convert_fusion = bf16[2048,4096]{1,0:T(8,128)(2,1)} fusion(bf16[1280,4096]{1,0:T(8,128)(2,1)} %param.7, bf16[2048,1280]{1,0:T(8,128)(2,1)S(1)} %fusion.8.clone.4), kind=kOutput, calls=%fused_computation.1 | convolution fusion | flops 21483225088 | bytes 32505856 | tf_op jit(solution)/shard_map/dot_general | solution.py:13
  179.0 0.1 reduce-scatter.2.cloned.1.call-update
  179.1 88.4 %reduce-scatter.2.cloned.1.call-done = bf16[256,4096]{1,0:T(8,128)(2,1)} async-done(((bf16[2048,4096]{1,0:T(8,128)(2,1)}), bf16[256,4096]{1,0:T(8,128)(2,1)}) %reduce-scatter.2.cloned.1.call-update) | async-done | bytes 2097168 | tf_op jit(solution)/shard_map/reduce_scatter | solution.py:14
Async XLA Ops:
  6.5 86.4 %all-gather.2.cloned.1.call-start = ((), (), s32[]{:S(2)}) async-start(), calls=%async_computation.1 | async-start | bytes 18874368 | tf_op jit(solution)/shard_map/all_gather | solution.py:9
  7.3 260.2 %reduce-scatter.2.cloned.1.call-start = ((), (), s32[]{:S(2)}) async-start(), calls=%async_computation.2 | async-start | bytes 18874368 | tf_op jit(solution)/shard_map/reduce_scatter | solution.py:14
  92.9 29.2 %copy-start = (bf16[2048,4096]{1,0:T(8,128)(2,1)S(1)}, bf16[2048,4096]{1,0:T(8,128)(2,1)}, u32[]{:S(2)}) copy-start(bf16[2048,4096]{1,0:T(8,128)(2,1)} %all-gather.2.cloned.1.call-done) | copy-start | bytes 50331652
Sparse Core Ops, SparseCore 0:
  8.9 83.9 all-gather.1
  179.2 88.2 reduce-scatter.1
where the time goes:
time: 274 us
  waiting for transfers between devices  175 us (64%)
  matrix products  86.1 us (31%)
  between operations  13.4 us (5%)
    reduce_scatter x1, waiting for transfers between devices, step(): return lax.psum_scatter(term, 'tp', scatter_dimension=0, tiled=True)  88.4 us
    all_gather x1, waiting for transfers between devices, step(): rows = lax.all_gather(x, 'tp', axis=0, tiled=True)  85.5 us
    dot_general x1, matrix products, step(): up = jnp.dot(rows, w_up, preferred_element_type=jnp.float32)  29.6 us
    dot_general x1, matrix products, step(): gate = jnp.dot(rows, w_gate, preferred_element_type=jnp.float32)  29.2 us
    dot_general x1, matrix products, step(): jnp.dot(hidden, w_down, preferred_element_type=jnp.float32)  27.2 us
  transfers between devices with their start and end apart: 2, of which 2 were waited for; matrix products, arithmetic and copies ran while one was open for 0% of the time, Pallas kernels for 0%

commit v1 on v0

v1 whole, which is shorter than its diff:
```python
import functools

import jax
import jax.numpy as jnp
from jax import lax
from jax.experimental import pallas as pl
from jax.experimental.pallas import tpu as pltpu
from jax.sharding import PartitionSpec as P

MESH = pl.DeviceIdType.MESH
FT = 256
NT = 512
OWN, NEAR, FAR, LAST = range(4)


def kernel(
    n, x, wg, wu, wd, y, xs, wgu, wds, h, rp, r3, stg,
    ag_send, ag_recv, d_send, d_recv, p_send, p_recv, r_send, r_recv, w_sem, wd_sem, x_sem, y_sem, credit,
):
    rows, depth = x.shape
    hidden = wg.shape[1]
    half, sub = rows // 2, rows // 4
    n_ft, n_nt = hidden // FT, depth // NT

    me = lax.axis_index("tp")
    core = lax.rem(me, 2)
    partner = me + 1 - 2 * core
    ahead = (lax.rem(me + 2, n), lax.rem(me + n - 2, n))

    def to(index):
        return dict(device_id={"tp": index}, device_id_type=MESH)

    barrier = pltpu.get_barrier_semaphore()
    for other in (*ahead, partner):
        pl.semaphore_signal(barrier, inc=1, **to(other))
    pl.semaphore_wait(barrier, 3)

    def piece(d, q):
        return pl.ds(d * half + q * sub, sub)

    def part_of(d):
        return pl.ds(d * half, half)

    def cols(t):
        return pl.ds(pl.multiple_of(t * NT, NT), NT)

    def gather(stage, d, q):
        src = {
            NEAR: x.at[piece(d, q)],
            FAR: xs.at[NEAR, core, piece(d, q)],
            LAST: x.at[piece(1 - d, q)],
        }[stage]
        return pltpu.make_async_remote_copy(
            src, xs.at[stage, core, piece(d, q)], ag_send.at[stage - 1, d, q], ag_recv.at[stage - 1, d, q], **to(ahead[d])
        )

    def share(stage, d, q):
        place = xs.at[stage, core, piece(d, q)]
        src = x.at[piece(d, q)] if stage == OWN else place
        return pltpu.make_async_remote_copy(src, place, d_send.at[stage, d, q], d_recv.at[stage, d, q], **to(partner))

    def trade(slot, src, t):
        return pltpu.make_async_remote_copy(
            src.at[:, cols(t)], rp.at[slot, :, cols(t)], p_send.at[slot, t], p_recv.at[slot, t], **to(partner)
        )

    def reduce(kind, d, t):
        src, dst = (
            (stg.at[part_of(1 - d), cols(t)], xs.at[OWN, 0, part_of(1 - d), cols(t)]),
            (xs.at[FAR, 1, part_of(d), cols(t)], xs.at[OWN, 1, part_of(1 - d), cols(t)]),
            (xs.at[LAST, 1, part_of(1 - d), cols(t)], r3.at[part_of(d), cols(t)]),
        )[kind]
        return pltpu.make_async_remote_copy(src, dst, r_send.at[kind, d, t], r_recv.at[kind, d, t], **to(ahead[d]))

    def load_x():
        return pltpu.make_async_copy(x, xs.at[OWN, core], x_sem)

    def load_w(j, which):
        src = (wg, wu)[which].at[:, pl.ds(pl.multiple_of(j * FT, FT), FT)]
        return pltpu.make_async_copy(src, wgu.at[j, :, pl.ds(which * FT, FT)], w_sem.at[which, j])

    def load_wd(t):
        return pltpu.make_async_copy(wd.at[:, cols(t)], wds.at[t], wd_sem.at[t])

    def store_y(t):
        return pltpu.make_async_copy(xs.at[NEAR, core, :, cols(t)], y.at[:, cols(t)], y_sem.at[t])

    pieces = [(d, q) for q in range(2) for d in range(2)]

    def up_stage(stage):
        @pl.loop(0, n_ft * 2)
        def _(i):
            j, m = i // 2, lax.rem(i, 2)
            if stage == OWN:

                @pl.when(m == 0)
                def _():
                    load_w(j, 0).wait()
                    load_w(j, 1).wait()

            both = jnp.dot(xs[stage, m], wgu[j], preferred_element_type=jnp.float32)
            value = (jax.nn.gelu(both[:, :FT]) * both[:, FT:]).astype(jnp.bfloat16)
            h[stage, m, :, pl.ds(pl.multiple_of(j * FT, FT), FT)] = value

    def term(stage, which, t):
        return jnp.dot(h[stage, which], wds[t], preferred_element_type=jnp.float32)

    def down_for_partner(stage, src, slot):
        @pl.loop(0, n_nt)
        def _(t):
            src[:, cols(t)] = term(stage, 1 - core, t).astype(jnp.bfloat16)
            trade(slot, src, t).start()

    def down_for_ring(stage, slot, dst, kind):
        @pl.loop(0, n_nt)
        def _(t):
            trade(slot, dst, t).wait_recv()
            total = term(stage, core, t) + rp[slot, :, cols(t)].astype(jnp.float32)
            if stage == LAST:
                for d in range(2):
                    reduce(1, d, t).wait_recv()
                total = total + xs[OWN, 1, :, cols(t)].astype(jnp.float32)
            dst[:, cols(t)] = total.astype(jnp.bfloat16)
            for d in range(2):
                reduce(kind, d, t).start()

    for d, q in pieces:
        gather(NEAR, d, q).start()
    load_x().start()
    for d, q in pieces:
        share(OWN, d, q).start()

    @pl.loop(0, n_ft)
    def _(j):
        load_w(j, 0).start()
        load_w(j, 1).start()

    @pl.loop(0, n_nt)
    def _(t):
        load_wd(t).start()

    load_x().wait()
    for d, q in pieces:
        share(OWN, d, q).wait_recv()
    up_stage(OWN)
    for other in ahead:
        pl.semaphore_signal(credit, inc=1, **to(other))

    for d, q in pieces:
        gather(NEAR, d, q).wait_recv()
        gather(FAR, d, q).start()
        share(NEAR, d, q).start()
    for d, q in pieces:
        gather(LAST, d, q).start()
    for d, q in pieces:
        share(NEAR, d, q).wait_recv()
    up_stage(NEAR)

    @pl.loop(0, n_nt)
    def _(t):
        load_wd(t).wait()

    spare = xs.at[NEAR, 1 - core]
    down_for_partner(NEAR, spare, 0)
    pl.semaphore_wait(credit, 2)
    down_for_ring(NEAR, 0, stg, 0)

    for d, q in pieces:
        gather(FAR, d, q).wait_recv()
        share(FAR, d, q).start()
    for d, q in pieces:
        share(FAR, d, q).wait()
    up_stage(FAR)
    down_for_partner(FAR, xs.at[FAR, 0], 1)
    down_for_ring(FAR, 1, xs.at[FAR, 1], 1)

    for d, q in pieces:
        gather(LAST, d, q).wait_recv()
        share(LAST, d, q).start()
    for d, q in pieces:
        share(LAST, d, q).wait()
    up_stage(LAST)

    @pl.loop(0, n_nt)
    def _(t):
        trade(0, spare, t).wait_send()
        trade(1, xs.at[FAR, 0], t).wait_send()

    down_for_partner(LAST, xs.at[LAST, 0], 0)
    down_for_partner(OWN, spare, 1)
    for d, q in pieces:
        share(OWN, d, q).wait_send()
        share(NEAR, d, q).wait_send()
        for stage in (NEAR, FAR, LAST):
            gather(stage, d, q).wait_send()
    down_for_ring(LAST, 0, xs.at[LAST, 1], 2)

    @pl.loop(0, n_nt)
    def _(t):
        trade(1, spare, t).wait_recv()
        total = term(OWN, core, t) + rp[1, :, cols(t)].astype(jnp.float32)
        for d in range(2):
            reduce(0, d, t).wait_recv()
        total = total + xs[OWN, 0, :, cols(t)].astype(jnp.float32)
        for d in range(2):
            reduce(2, d, t).wait_recv()
        total = total + r3[:, cols(t)].astype(jnp.float32)
        xs[NEAR, core, :, cols(t)] = total.astype(jnp.bfloat16)
        store_y(t).start()

    @pl.loop(0, n_nt)
    def _(t):
        trade(0, xs.at[LAST, 0], t).wait_send()
        trade(1, spare, t).wait_send()
        for kind in range(3):
            for d in range(2):
                reduce(kind, d, t).wait_send()
        store_y(t).wait()


def solution(mesh):
    n = mesh.shape["tp"]

    def step(x, w_gate, w_up, w_down):
        rows, depth = x.shape
        hidden = w_gate.shape[1]
        n_ft, n_nt = hidden // FT, depth // NT
        dma = pltpu.SemaphoreType.DMA
        any_space = pl.BlockSpec(memory_space=pl.ANY)
        flops = 6 * n * rows * depth * hidden
        return pl.pallas_call(
            functools.partial(kernel, n),
            out_shape=jax.ShapeDtypeStruct((rows, depth), jnp.bfloat16),
            in_specs=[any_space] * 4,
            out_specs=any_space,
            scratch_shapes=[
                pltpu.VMEM((4, 2, rows, depth), jnp.bfloat16),
                pltpu.VMEM((n_ft, depth, 2 * FT), jnp.bfloat16),
                pltpu.VMEM((n_nt, hidden, NT), jnp.bfloat16),
                pltpu.VMEM((4, 2, rows, hidden), jnp.bfloat16),
                pltpu.VMEM((2, rows, depth), jnp.bfloat16),
                pltpu.VMEM((rows, depth), jnp.bfloat16),
                pltpu.VMEM((rows, depth), jnp.bfloat16),
                dma((3, 2, 2)),
                dma((3, 2, 2)),
                dma((4, 2, 2)),
                dma((4, 2, 2)),
                dma((2, n_nt)),
                dma((2, n_nt)),
                dma((3, 2, n_nt)),
                dma((3, 2, n_nt)),
                dma((2, n_ft)),
                dma((n_nt,)),
                dma,
                dma((n_nt,)),
                pltpu.SemaphoreType.REGULAR,
            ],
            compiler_params=pltpu.CompilerParams(
                collective_id=0, has_side_effects=True, vmem_limit_bytes=67043328
            ),
            cost_estimate=pl.CostEstimate(flops=flops, bytes_accessed=6 * depth * hidden, transcendentals=0),
        )(x, w_gate, w_up, w_down)

    return jax.shard_map(
        step,
        mesh=mesh,
        in_specs=(P(("dp", "tp"), None), P(None, "tp"), P(None, "tp"), P("tp", None)),
        out_specs=P(("dp", "tp"), None),
        check_vma=False,
    )
```

time: 274 us -> 146 us (0.53)
  waiting for transfers between devices: 175 us -> 0 us
  Pallas kernels: 0 us -> 143 us
  matrix products: 86.1 us -> 0 us
  between operations: 13.4 us -> 0.01 us
  local copies, waits for them, and re-layouts: 0.01 us -> 3.13 us
    pallas_call x0 -> x1, Pallas kernels: none -> 143 us  [step(): pl.pallas_call(functools.partial(kernel, n), out_shape=jax.ShapeDtypeStru...]
    reduce_scatter x1 -> x0, waiting for transfers between devices: 88.4 us -> none  [step(): return lax.psum_scatter(term, 'tp', scatter_dimension=0, tiled=True)]
    dot_general x3 -> x0, matrix products: 86.1 us -> none  [the longest x1 29.6 us: step(): up = jnp.dot(rows, w_up, preferred_element_type=jnp.float32)]
    all_gather x1 -> x0, waiting for transfers between devices: 85.5 us -> none  [step(): rows = lax.all_gather(x, 'tp', axis=0, tiled=True)]
    unnamed x2 -> x1, local copies, waits for them, and re-layouts: 0.01 us -> 3.13 us
  transfers between devices with their start and end apart: 2 -> 0, of which waited for: 2 -> 0; matrix products, arithmetic and copies ran while one was open for 0% -> 0% of each run, Pallas kernels for 0% -> 0%
where the time goes in v1:
time: 146 us
  Pallas kernels  143 us (98%)
  local copies, waits for them, and re-layouts  3.13 us (2%)
    pallas_call x1, Pallas kernels, step(): pl.pallas_call(functools.partial(kernel, n), out_shape=jax.ShapeDtypeStru...  143 us
    unnamed x1, local copies, waits for them, and re-layouts  3.13 us

profile of v1, /device:TPU:112, one launch (start us, length us, event | category | flops | bytes accessed | tf_op | source)
XLA Modules:
  0.0 145.9 jit_solution(4239593599666341334)
XLA Ops:
  0.0 142.8 %shard_map.46 = bf16[256,4096]{1,0:T(8,128)(2,1)} custom-call(bf16[256,4096]{1,0:T(8,128)(2,1)} %x.1, bf16[4096,1280]{1,0:T(8,128)(2,1)} %wg.1, bf16[4096,1280]{1,0:T(8,128)(2,1)} %wu.1, bf16[1280,4096]{1,0:T(8,128)(2,1)} %wd.1), custom_call_target="tpu_custom_call" | custom-call | flops 64424509440 | bytes 31457280 | tf_op jit(solution)/shard_map/pallas_call | solution.py:231
  142.8 3.1 %copy.6 = bf16[256,4096]{1,0:T(8,128)(2,1)} copy(bf16[256,4096]{1,0:T(8,128)(2,1)} %shard_map.46) | data formatting | bytes 4194304

commit v2 on v1

--- a/solution.py
+++ b/solution.py
@@ -10,12 +10,13 @@
 MESH = pl.DeviceIdType.MESH
 FT = 256
 NT = 512
+CHUNKS = ((8,), (4, 4), (4, 2, 1, 1))
 OWN, NEAR, FAR, LAST = range(4)
 
 
 def kernel(
     n, x, wg, wu, wd, y, xs, wgu, wds, h, rp, r3, stg,
-    ag_send, ag_recv, d_send, d_recv, p_send, p_recv, r_send, r_recv, w_sem, wd_sem, x_sem, y_sem, credit,
+    ag_send, ag_recv, d_send, d_recv, p_send, p_recv, r_send, r_recv, w_sem, wd_sem, x_sem, credit,
 ):
     rows, depth = x.shape
     hidden = wg.shape[1]
@@ -44,14 +45,15 @@
     def cols(t):
         return pl.ds(pl.multiple_of(t * NT, NT), NT)
 
-    def gather(stage, d, q):
+    def gather(stage, d, q=0):
+        place = part_of(d) if stage == LAST else piece(d, q)
         src = {
-            NEAR: x.at[piece(d, q)],
-            FAR: xs.at[NEAR, core, piece(d, q)],
-            LAST: x.at[piece(1 - d, q)],
+            NEAR: x.at[place],
+            FAR: xs.at[NEAR, core, place],
+            LAST: x.at[part_of(1 - d)],
         }[stage]
         return pltpu.make_async_remote_copy(
-            src, xs.at[stage, core, piece(d, q)], ag_send.at[stage - 1, d, q], ag_recv.at[stage - 1, d, q], **to(ahead[d])
+            src, xs.at[stage, core, place], ag_send.at[stage - 1, d, q], ag_recv.at[stage - 1, d, q], **to(ahead[d])
         )
 
     def share(stage, d, q):
@@ -64,13 +66,31 @@
             src.at[:, cols(t)], rp.at[slot, :, cols(t)], p_send.at[slot, t], p_recv.at[slot, t], **to(partner)
         )
 
-    def reduce(kind, d, t):
+    def reduce(kind, d, i):
+        first = sum(CHUNKS[kind][:i])
+        some = pl.ds(first * NT, CHUNKS[kind][i] * NT)
         src, dst = (
-            (stg.at[part_of(1 - d), cols(t)], xs.at[OWN, 0, part_of(1 - d), cols(t)]),
-            (xs.at[FAR, 1, part_of(d), cols(t)], xs.at[OWN, 1, part_of(1 - d), cols(t)]),
-            (xs.at[LAST, 1, part_of(1 - d), cols(t)], r3.at[part_of(d), cols(t)]),
+            (stg.at[part_of(1 - d), some], xs.at[OWN, 0, part_of(1 - d), some]),
+            (xs.at[FAR, 1, part_of(d), some], xs.at[OWN, 1, part_of(1 - d), some]),
+            (xs.at[LAST, 1, part_of(1 - d), some], r3.at[part_of(d), some]),
         )[kind]
-        return pltpu.make_async_remote_copy(src, dst, r_send.at[kind, d, t], r_recv.at[kind, d, t], **to(ahead[d]))
+        return pltpu.make_async_remote_copy(src, dst, r_send.at[kind, d, i], r_recv.at[kind, d, i], **to(ahead[d]))
+
+    def await_sums(kind, t):
+        for i in range(len(CHUNKS[kind])):
+
+            @pl.when(t == sum(CHUNKS[kind][:i]))
+            def _(i=i):
+                for d in range(2):
+                    reduce(kind, d, i).wait_recv()
+
+    def send_sums(kind, t):
+        for i in range(len(CHUNKS[kind])):
+
+            @pl.when(t == sum(CHUNKS[kind][: i + 1]) - 1)
+            def _(i=i):
+                for d in range(2):
+                    reduce(kind, d, i).start()
 
     def load_x():
         return pltpu.make_async_copy(x, xs.at[OWN, core], x_sem)
@@ -81,9 +101,6 @@
 
     def load_wd(t):
         return pltpu.make_async_copy(wd.at[:, cols(t)], wds.at[t], wd_sem.at[t])
-
-    def store_y(t):
-        return pltpu.make_async_copy(xs.at[NEAR, core, :, cols(t)], y.at[:, cols(t)], y_sem.at[t])
 
     pieces = [(d, q) for q in range(2) for d in range(2)]
 
@@ -117,12 +134,10 @@
             trade(slot, dst, t).wait_recv()
             total = term(stage, core, t) + rp[slot, :, cols(t)].astype(jnp.float32)
             if stage == LAST:
-                for d in range(2):
-                    reduce(1, d, t).wait_recv()
+                await_sums(1, t)
                 total = total + xs[OWN, 1, :, cols(t)].astype(jnp.float32)
             dst[:, cols(t)] = total.astype(jnp.bfloat16)
-            for d in range(2):
-                reduce(kind, d, t).start()
+            send_sums(kind, t)
 
     for d, q in pieces:
         gather(NEAR, d, q).start()
@@ -150,8 +165,8 @@
         gather(NEAR, d, q).wait_recv()
         gather(FAR, d, q).start()
         share(NEAR, d, q).start()
-    for d, q in pieces:
-        gather(LAST, d, q).start()
+    for d in range(2):
+        gather(LAST, d).start()
     for d, q in pieces:
         share(NEAR, d, q).wait_recv()
     up_stage(NEAR)
@@ -174,8 +189,9 @@
     down_for_partner(FAR, xs.at[FAR, 0], 1)
     down_for_ring(FAR, 1, xs.at[FAR, 1], 1)
 
-    for d, q in pieces:
-        gather(LAST, d, q).wait_recv()
+    for d in range(2):
+        gather(LAST, d).wait_recv()
+    for d, q in pieces:
         share(LAST, d, q).start()
     for d, q in pieces:
         share(LAST, d, q).wait()
@@ -191,31 +207,31 @@
     for d, q in pieces:
         share(OWN, d, q).wait_send()
         share(NEAR, d, q).wait_send()
-        for stage in (NEAR, FAR, LAST):
-            gather(stage, d, q).wait_send()
+        gather(NEAR, d, q).wait_send()
+        gather(FAR, d, q).wait_send()
+    for d in range(2):
+        gather(LAST, d).wait_send()
     down_for_ring(LAST, 0, xs.at[LAST, 1], 2)
 
     @pl.loop(0, n_nt)
     def _(t):
         trade(1, spare, t).wait_recv()
         total = term(OWN, core, t) + rp[1, :, cols(t)].astype(jnp.float32)
-        for d in range(2):
-            reduce(0, d, t).wait_recv()
+        await_sums(0, t)
         total = total + xs[OWN, 0, :, cols(t)].astype(jnp.float32)
-        for d in range(2):
-            reduce(2, d, t).wait_recv()
+        await_sums(2, t)
         total = total + r3[:, cols(t)].astype(jnp.float32)
-        xs[NEAR, core, :, cols(t)] = total.astype(jnp.bfloat16)
-        store_y(t).start()
+        y[:, cols(t)] = total.astype(jnp.bfloat16)
 
     @pl.loop(0, n_nt)
     def _(t):
         trade(0, xs.at[LAST, 0], t).wait_send()
         trade(1, spare, t).wait_send()
-        for kind in range(3):
+
+    for kind in range(3):
+        for i in range(len(CHUNKS[kind])):
             for d in range(2):
-                reduce(kind, d, t).wait_send()
-        store_y(t).wait()
+                reduce(kind, d, i).wait_send()
 
 
 def solution(mesh):
@@ -230,9 +246,9 @@
         flops = 6 * n * rows * depth * hidden
         return pl.pallas_call(
             functools.partial(kernel, n),
-            out_shape=jax.ShapeDtypeStruct((rows, depth), jnp.bfloat16),
+            out_shape=pltpu.VMEM((rows, depth), jnp.bfloat16),
             in_specs=[any_space] * 4,
-            out_specs=any_space,
+            out_specs=pl.BlockSpec(memory_space=pltpu.VMEM),
             scratch_shapes=[
                 pltpu.VMEM((4, 2, rows, depth), jnp.bfloat16),
                 pltpu.VMEM((n_ft, depth, 2 * FT), jnp.bfloat16),
@@ -247,20 +263,18 @@
                 dma((4, 2, 2)),
                 dma((2, n_nt)),
                 dma((2, n_nt)),
-                dma((3, 2, n_nt)),
-                dma((3, 2, n_nt)),
+                dma((3, 2, len(CHUNKS[2]))),
+                dma((3, 2, len(CHUNKS[2]))),
                 dma((2, n_ft)),
                 dma((n_nt,)),
                 dma,
-                dma((n_nt,)),
                 pltpu.SemaphoreType.REGULAR,
             ],
             compiler_params=pltpu.CompilerParams(
-                collective_id=0, has_side_effects=True, vmem_limit_bytes=67043328
+                collective_id=0, has_side_effects=True, vmem_limit_bytes=61 * 2**20
             ),
             cost_estimate=pl.CostEstimate(flops=flops, bytes_accessed=6 * depth * hidden, transcendentals=0),
         )(x, w_gate, w_up, w_down)
-
     return jax.shard_map(
         step,
         mesh=mesh,

time: 146 us -> 143 us (0.979)
  local copies, waits for them, and re-layouts: 3.13 us -> 1.32 us
    unnamed x1, local copies, waits for them, and re-layouts: 3.13 us -> 1.32 us
where the time goes in v2:
time: 143 us
  Pallas kernels  142 us (99%)
    pallas_call x1, Pallas kernels, step(): pl.pallas_call(functools.partial(kernel, n), out_shape=pltpu.VMEM((rows,...  142 us

profile of v2, /device:TPU:112, one launch (start us, length us, event | category | flops | bytes accessed | tf_op | source)
XLA Modules:
  0.0 142.9 jit_solution(1144141447587199268)
XLA Ops:
  0.0 141.6 %shard_map.46 = bf16[256,4096]{1,0:T(8,128)(2,1)S(1)} custom-call(bf16[256,4096]{1,0:T(8,128)(2,1)} %x.1, bf16[4096,1280]{1,0:T(8,128)(2,1)} %wg.1, bf16[4096,1280]{1,0:T(8,128)(2,1)} %wu.1, bf16[1280,4096]{1,0:T(8,128)(2,1)} %wd.1), custom_call_target="tpu_custom_call" | custom-call | flops 64424509440 | bytes 31457280 | tf_op jit(solution)/shard_map/pallas_call | solution.py:247
  141.6 1.3 copy.6

commit v3 on v0

v3 whole, which is shorter than its diff:
```python
import functools

import jax
import jax.numpy as jnp
from jax import lax
from jax.experimental import pallas as pl
from jax.experimental.pallas import tpu as pltpu
from jax.sharding import PartitionSpec as P

MESH = pl.DeviceIdType.MESH
FT = 256
NT = 512
FAR_PARTS = (4, 4)
LAST_PARTS = (4, 3, 1)
OWN, NEAR, FAR, LAST = range(4)


def kernel(
    n, x, wg, wu, wd, y, xs, wgu, wds, h, rp, rf, stg,
    g_send, g_recv, d_send, d_recv, p_send, p_recv, n_send, n_recv, f_send, f_recv, l_send, l_recv,
    w_sem, wd_sem, x_sem, ready, credit, late_credit,
):
    rows, depth = x.shape
    hidden = wg.shape[1]
    half = rows // 2
    n_ft, n_nt = hidden // FT, depth // NT

    me = lax.axis_index("tp")
    core = lax.rem(me, 2)
    other = 1 - core
    way = other
    partner = me + 1 - 2 * core
    ahead = lax.rem(me + 4 * core - 2 + n, n)
    behind = lax.rem(me + 2 - 4 * core + n, n)
    beside = ahead + 1 - 2 * core

    def to(index):
        return dict(device_id={"tp": index}, device_id_type=MESH)

    def block(i):
        return pl.ds(pl.multiple_of(i * half, half), half)

    def cols(t, steps=1):
        return pl.ds(pl.multiple_of(t * NT, NT), steps * NT)

    def gather(stage, i):
        origin = (core, other)[i]
        part = block(1 - way if stage == LAST else way)
        src = xs.at[NEAR, way, block(origin)] if stage == FAR else (x.at[part], xs.at[OWN, other, part])[i]
        dst = xs.at[stage, way, block(origin)]
        return pltpu.make_async_remote_copy(src, dst, g_send.at[stage, i], g_recv.at[stage, i], **to(ahead))

    def share(stage, i):
        if stage == OWN:
            part = block((core, other)[i])
            src, dst = x.at[part], xs.at[OWN, core, part]
        else:
            src = dst = xs.at[stage, way, block((core, other)[i])]
        return pltpu.make_async_remote_copy(src, dst, d_send.at[stage, i], d_recv.at[stage, i], **to(partner))

    def trade(slot, src, t):
        return pltpu.make_async_remote_copy(
            src.at[:, cols(t)], rp.at[slot, :, cols(t)], p_send.at[slot, t], p_recv.at[slot, t], **to(partner)
        )

    def near_sum(owner, sent=None):
        sent = way if sent is None else sent
        return pltpu.make_async_remote_copy(
            stg.at[block(owner)], xs.at[OWN, owner, block(1 - sent)],
            n_send.at[owner], n_recv.at[sent], **to(ahead - core + owner),
        )

    def far_sum(i):
        some = pl.ds(sum(FAR_PARTS[:i]) * NT, FAR_PARTS[i] * NT)
        return pltpu.make_async_remote_copy(xs.at[FAR, 1, :, some], rf.at[:, some], f_send.at[i], f_recv.at[i], **to(ahead))

    def last_sum(i, owner, sent=None):
        sent = way if sent is None else sent
        some = pl.ds(sum(LAST_PARTS[:i]) * NT, LAST_PARTS[i] * NT)
        return pltpu.make_async_remote_copy(
            xs.at[LAST, 1, block(owner), some], xs.at[OWN, 1 - owner, block(sent), some],
            l_send.at[i, owner], l_recv.at[i, sent], **to(ahead - core + owner),
        )

    def at_start(parts, t, act):
        for i in range(len(parts)):
            pl.when(t == sum(parts[:i]))(functools.partial(act, i))

    def at_end(parts, t, act):
        for i in range(len(parts)):
            pl.when(t == sum(parts[: i + 1]) - 1)(functools.partial(act, i))

    def load_x():
        return pltpu.make_async_copy(x, xs.at[OWN, core], x_sem)

    def load_w(j, which):
        src = (wg, wu)[which].at[:, pl.ds(pl.multiple_of(j * FT, FT), FT)]
        return pltpu.make_async_copy(src, wgu.at[j, :, pl.ds(which * FT, FT)], w_sem.at[which, j])

    def load_wd(t):
        return pltpu.make_async_copy(wd.at[:, cols(t)], wds.at[t], wd_sem.at[t])

    def up_stage(stage):
        @pl.loop(0, n_ft * 2)
        def _(i):
            j, m = i // 2, lax.rem(i, 2)
            if stage == OWN:

                @pl.when(m == 0)
                def _():
                    load_w(j, 0).wait()
                    load_w(j, 1).wait()

            both = jnp.dot(xs[stage, m], wgu[j], preferred_element_type=jnp.float32)
            value = (jax.nn.gelu(both[:, :FT]) * both[:, FT:]).astype(jnp.bfloat16)
            h[stage, m, :, pl.ds(pl.multiple_of(j * FT, FT), FT)] = value

    def term(stage, which, t):
        return jnp.dot(h[stage, which], wds[t], preferred_element_type=jnp.float32)

    def down_for_partner(stage, which, src, slot):
        @pl.loop(0, n_nt)
        def _(t):
            src[:, cols(t)] = term(stage, which, t).astype(jnp.bfloat16)
            trade(slot, src, t).start()

    def chip_sum(stage, which, slot, t):
        trade(slot, spare, t).wait_recv()
        return term(stage, which, t) + rp[slot, :, cols(t)].astype(jnp.float32)

    spare = xs.at[NEAR, core]

    barrier = pltpu.get_barrier_semaphore()
    pl.semaphore_signal(barrier, inc=1, **to(behind))

    @pl.when(core == 1)
    def _():
        pl.semaphore_signal(barrier, inc=1, **to(partner))
        pl.semaphore_wait(barrier, 1)

    @pl.when(core == 0)
    def _():
        pl.semaphore_wait(barrier, 2)

    gather(NEAR, 0).start()
    load_x().start()

    @pl.when(core == 0)
    def _():
        pl.semaphore_signal(ready, inc=1, **to(partner))

    @pl.loop(0, n_ft)
    def _(j):
        load_w(j, 0).start()
        load_w(j, 1).start()

    @pl.loop(0, n_nt)
    def _(t):
        load_wd(t).start()

    @pl.when(core == 1)
    def _():
        pl.semaphore_wait(ready, 1)

    for i in range(2):
        share(OWN, i).start()
    share(OWN, 0).wait_recv()
    share(OWN, 1).wait_recv()
    gather(NEAR, 1).start()
    load_x().wait()
    up_stage(OWN)

    for i in range(2):
        gather(NEAR, i).wait_recv()
        gather(FAR, i).start()
        share(NEAR, i).start()
    for i in range(2):
        gather(LAST, i).start()
    for i in range(2):
        share(NEAR, i).wait_recv()
    for writer in (behind, beside):
        pl.semaphore_signal(credit, inc=1, **to(writer))
    up_stage(NEAR)

    @pl.loop(0, n_nt)
    def _(t):
        load_wd(t).wait()

    down_for_partner(NEAR, other, spare, 0)

    @pl.loop(0, n_nt)
    def _(t):
        stg[:, cols(t)] = chip_sum(NEAR, core, 0, t).astype(jnp.bfloat16)

    pl.semaphore_wait(credit, 2)
    for owner in range(2):
        near_sum(owner).start()

    for i in range(2):
        gather(FAR, i).wait_recv()
        share(FAR, i).start()
    for i in range(2):
        share(FAR, i).wait()
    up_stage(FAR)
    down_for_partner(FAR, core, xs.at[FAR, 0], 1)

    @pl.loop(0, n_nt)
    def _(t):
        xs[FAR, 1, :, cols(t)] = chip_sum(FAR, other, 1, t).astype(jnp.bfloat16)
        at_end(FAR_PARTS, t, lambda i: far_sum(i).start())

    for i in range(2):
        gather(LAST, i).wait_recv()
        share(LAST, i).start()
    for i in range(2):
        gather(LAST, i).wait_send()
        gather(NEAR, i).wait_send()
    for writer in (behind, beside):
        pl.semaphore_signal(late_credit, inc=1, **to(writer))
    for i in range(2):
        share(LAST, i).wait()
    up_stage(LAST)

    @pl.loop(0, n_nt)
    def _(t):
        trade(0, spare, t).wait_send()
        trade(1, xs.at[FAR, 0], t).wait_send()

    down_for_partner(LAST, other, xs.at[LAST, 0], 0)
    down_for_partner(OWN, other, spare, 1)
    pl.semaphore_wait(late_credit, 2)

    def send_last(i):
        for owner in range(2):
            last_sum(i, owner).start()

    @pl.loop(0, n_nt)
    def _(t):
        total = chip_sum(LAST, core, 0, t)
        at_start(FAR_PARTS, t, lambda i: far_sum(i).wait_recv())
        total = total + rf[:, cols(t)].astype(jnp.float32)
        xs[LAST, 1, :, cols(t)] = total.astype(jnp.bfloat16)
        at_end(LAST_PARTS, t, send_last)

    for sent in range(2):
        near_sum(core, sent).wait_recv()

    def await_last(i):
        for sent in range(2):
            last_sum(i, core, sent).wait_recv()

    @pl.loop(0, n_nt)
    def _(t):
        total = chip_sum(OWN, core, 1, t) + xs[OWN, core, :, cols(t)].astype(jnp.float32)
        at_start(LAST_PARTS, t, await_last)
        total = total + xs[OWN, other, :, cols(t)].astype(jnp.float32)
        y[:, cols(t)] = total.astype(jnp.bfloat16)

    @pl.loop(0, n_nt)
    def _(t):
        trade(0, xs.at[LAST, 0], t).wait_send()
        trade(1, spare, t).wait_send()

    for i in range(2):
        gather(FAR, i).wait_send()
        share(OWN, i).wait_send()
        share(NEAR, i).wait_send()
        near_sum(i).wait_send()
    for i in range(len(FAR_PARTS)):
        far_sum(i).wait_send()
    for i in range(len(LAST_PARTS)):
        for owner in range(2):
            last_sum(i, owner).wait_send()


def solution(mesh):
    n = mesh.shape["tp"]

    def step(x, w_gate, w_up, w_down):
        rows, depth = x.shape
        hidden = w_gate.shape[1]
        n_ft, n_nt = hidden // FT, depth // NT
        dma, plain = pltpu.SemaphoreType.DMA, pltpu.SemaphoreType.REGULAR
        any_space = pl.BlockSpec(memory_space=pl.ANY)
        return pl.pallas_call(
            functools.partial(kernel, n),
            out_shape=pltpu.VMEM((rows, depth), jnp.bfloat16),
            in_specs=[any_space] * 4,
            out_specs=pl.BlockSpec(memory_space=pltpu.VMEM),
            scratch_shapes=[
                pltpu.VMEM((4, 2, rows, depth), jnp.bfloat16),
                pltpu.VMEM((n_ft, depth, 2 * FT), jnp.bfloat16),
                pltpu.VMEM((n_nt, hidden, NT), jnp.bfloat16),
                pltpu.VMEM((4, 2, rows, hidden), jnp.bfloat16),
                pltpu.VMEM((2, rows, depth), jnp.bfloat16),
                pltpu.VMEM((rows, depth), jnp.bfloat16),
                pltpu.VMEM((rows, depth), jnp.bfloat16),
                dma((4, 2)),
                dma((4, 2)),
                dma((4, 2)),
                dma((4, 2)),
                dma((2, n_nt)),
                dma((2, n_nt)),
                dma((2,)),
                dma((2,)),
                dma((len(FAR_PARTS),)),
                dma((len(FAR_PARTS),)),
                dma((len(LAST_PARTS), 2)),
                dma((len(LAST_PARTS), 2)),
                dma((2, n_ft)),
                dma((n_nt,)),
                dma,
                plain,
                plain,
                plain,
            ],
            compiler_params=pltpu.CompilerParams(
                collective_id=0, has_side_effects=True, vmem_limit_bytes=61 * 2**20
            ),
            cost_estimate=pl.CostEstimate(
                flops=6 * n * rows * depth * hidden, bytes_accessed=6 * depth * hidden, transcendentals=0
            ),
        )(x, w_gate, w_up, w_down)

    return jax.shard_map(
        step,
        mesh=mesh,
        in_specs=(P(("dp", "tp"), None), P(None, "tp"), P(None, "tp"), P("tp", None)),
        out_specs=P(("dp", "tp"), None),
        check_vma=False,
    )
```

time: 274 us -> 142 us (0.52)
  waiting for transfers between devices: 175 us -> 0 us
  Pallas kernels: 0 us -> 141 us
  matrix products: 86.1 us -> 0 us
  between operations: 13.4 us -> 0.01 us
    pallas_call x0 -> x1, Pallas kernels: none -> 141 us  [step(): pl.pallas_call(functools.partial(kernel, n), out_shape=pltpu.VMEM((rows,...]
    reduce_scatter x1 -> x0, waiting for transfers between devices: 88.4 us -> none  [step(): return lax.psum_scatter(term, 'tp', scatter_dimension=0, tiled=True)]
    dot_general x3 -> x0, matrix products: 86.1 us -> none  [the longest x1 29.6 us: step(): up = jnp.dot(rows, w_up, preferred_element_type=jnp.float32)]
    all_gather x1 -> x0, waiting for transfers between devices: 85.5 us -> none  [step(): rows = lax.all_gather(x, 'tp', axis=0, tiled=True)]
  transfers between devices with their start and end apart: 2 -> 0, of which waited for: 2 -> 0; matrix products, arithmetic and copies ran while one was open for 0% -> 0% of each run, Pallas kernels for 0% -> 0%
where the time goes in v3:
time: 142 us
  Pallas kernels  141 us (99%)
    pallas_call x1, Pallas kernels, step(): pl.pallas_call(functools.partial(kernel, n), out_shape=pltpu.VMEM((rows,...  141 us

profile of v3, /device:TPU:112, one launch (start us, length us, event | category | flops | bytes accessed | tf_op | source)
XLA Modules:
  0.0 142.1 jit_solution(9290377595617569864)
XLA Ops:
  0.0 140.7 %shard_map.46 = bf16[256,4096]{1,0:T(8,128)(2,1)S(1)} custom-call(bf16[256,4096]{1,0:T(8,128)(2,1)} %x.1, bf16[4096,1280]{1,0:T(8,128)(2,1)} %wg.1, bf16[4096,1280]{1,0:T(8,128)(2,1)} %wu.1, bf16[1280,4096]{1,0:T(8,128)(2,1)} %wd.1), custom_call_target="tpu_custom_call" | custom-call | flops 64424509440 | bytes 31457280 | tf_op jit(solution)/shard_map/pallas_call | solution.py:285
  140.7 1.3 copy.6

commit v4 on v3

--- a/solution.py
+++ b/solution.py
@@ -245,17 +245,6 @@
     for sent in range(2):
         near_sum(core, sent).wait_recv()
 
-    def await_last(i):
-        for sent in range(2):
-            last_sum(i, core, sent).wait_recv()
-
-    @pl.loop(0, n_nt)
-    def _(t):
-        total = chip_sum(OWN, core, 1, t) + xs[OWN, core, :, cols(t)].astype(jnp.float32)
-        at_start(LAST_PARTS, t, await_last)
-        total = total + xs[OWN, other, :, cols(t)].astype(jnp.float32)
-        y[:, cols(t)] = total.astype(jnp.bfloat16)
-
     @pl.loop(0, n_nt)
     def _(t):
         trade(0, xs.at[LAST, 0], t).wait_send()
@@ -268,9 +257,23 @@
         near_sum(i).wait_send()
     for i in range(len(FAR_PARTS)):
         far_sum(i).wait_send()
-    for i in range(len(LAST_PARTS)):
+
+    def await_last(i):
         for owner in range(2):
-            last_sum(i, owner).wait_send()
+            if i > 0:
+                last_sum(i - 1, owner).wait_send()
+        for sent in range(2):
+            last_sum(i, core, sent).wait_recv()
+
+    @pl.loop(0, n_nt)
+    def _(t):
+        total = chip_sum(OWN, core, 1, t) + xs[OWN, core, :, cols(t)].astype(jnp.float32)
+        at_start(LAST_PARTS, t, await_last)
+        total = total + xs[OWN, other, :, cols(t)].astype(jnp.float32)
+        y[:, cols(t)] = total.astype(jnp.bfloat16)
+
+    for owner in range(2):
+        last_sum(len(LAST_PARTS) - 1, owner).wait_send()
 
 
 def solution(mesh):

time: 142 us -> 142 us (level)
  no operation moved by 1% of the time
where the time goes in v4:
time: 142 us
  Pallas kernels  141 us (99%)
    pallas_call x1, Pallas kernels, step(): pl.pallas_call(functools.partial(kernel, n), out_shape=pltpu.VMEM((rows,...  141 us

profile of v4, /device:TPU:112, one launch (start us, length us, event | category | flops | bytes accessed | tf_op | source)
XLA Modules:
  0.0 142.1 jit_solution(17553306330229610720)
XLA Ops:
  0.0 140.7 %shard_map.46 = bf16[256,4096]{1,0:T(8,128)(2,1)S(1)} custom-call(bf16[256,4096]{1,0:T(8,128)(2,1)} %x.1, bf16[4096,1280]{1,0:T(8,128)(2,1)} %wg.1, bf16[4096,1280]{1,0:T(8,128)(2,1)} %wu.1, bf16[1280,4096]{1,0:T(8,128)(2,1)} %wd.1), custom_call_target="tpu_custom_call" | custom-call | flops 64424509440 | bytes 31457280 | tf_op jit(solution)/shard_map/pallas_call | solution.py:288
  140.7 1.3 copy.6

commit v5 on v3

--- a/solution.py
+++ b/solution.py
@@ -11,6 +11,7 @@
 FT = 256
 NT = 512
 FAR_PARTS = (4, 4)
+TRADE_PARTS = (4, 4)
 LAST_PARTS = (4, 3, 1)
 OWN, NEAR, FAR, LAST = range(4)
 
@@ -48,7 +49,11 @@
         part = block(1 - way if stage == LAST else way)
         src = xs.at[NEAR, way, block(origin)] if stage == FAR else (x.at[part], xs.at[OWN, other, part])[i]
         dst = xs.at[stage, way, block(origin)]
-        return pltpu.make_async_remote_copy(src, dst, g_send.at[stage, i], g_recv.at[stage, i], **to(ahead))
+        return pltpu.make_async_remote_copy(src, dst, g_send.at[stage - 1], g_recv.at[stage - 1, i], **to(ahead))
+
+    def gathered(stage):
+        both = xs.at[stage, way]
+        return pltpu.make_async_remote_copy(both, both, g_send.at[stage - 1], g_recv.at[stage - 1, 0], **to(ahead))
 
     def share(stage, i):
         if stage == OWN:
@@ -56,31 +61,44 @@
             src, dst = x.at[part], xs.at[OWN, core, part]
         else:
             src = dst = xs.at[stage, way, block((core, other)[i])]
-        return pltpu.make_async_remote_copy(src, dst, d_send.at[stage, i], d_recv.at[stage, i], **to(partner))
-
-    def trade(slot, src, t):
+        return pltpu.make_async_remote_copy(src, dst, d_send.at[stage], d_recv.at[stage], **to(partner))
+
+    def shared(stage):
+        src, dst = (x, xs.at[OWN, core]) if stage == OWN else (xs.at[stage, way],) * 2
+        return pltpu.make_async_remote_copy(src, dst, d_send.at[stage], d_recv.at[stage], **to(partner))
+
+    def trade(slot, src, i):
+        some = pl.ds(sum(TRADE_PARTS[:i]) * NT, TRADE_PARTS[i] * NT)
         return pltpu.make_async_remote_copy(
-            src.at[:, cols(t)], rp.at[slot, :, cols(t)], p_send.at[slot, t], p_recv.at[slot, t], **to(partner)
+            src.at[:, some], rp.at[slot, :, some], p_send.at[slot], p_recv.at[slot, i], **to(partner)
         )
 
-    def near_sum(owner, sent=None):
-        sent = way if sent is None else sent
-        return pltpu.make_async_remote_copy(
-            stg.at[block(owner)], xs.at[OWN, owner, block(1 - sent)],
-            n_send.at[owner], n_recv.at[sent], **to(ahead - core + owner),
-        )
+    def traded(slot, src):
+        return pltpu.make_async_remote_copy(src, rp.at[slot], p_send.at[slot], p_recv.at[slot, 0], **to(partner))
+
+    def near_sum(owner):
+        dst = xs.at[OWN, owner, block(1 - way)]
+        return pltpu.make_async_remote_copy(stg.at[block(owner)], dst, n_send, n_recv, **to(ahead - core + owner))
+
+    def near_sums():
+        return pltpu.make_async_remote_copy(stg, xs.at[OWN, core], n_send, n_recv, **to(ahead))
 
     def far_sum(i):
         some = pl.ds(sum(FAR_PARTS[:i]) * NT, FAR_PARTS[i] * NT)
-        return pltpu.make_async_remote_copy(xs.at[FAR, 1, :, some], rf.at[:, some], f_send.at[i], f_recv.at[i], **to(ahead))
-
-    def last_sum(i, owner, sent=None):
-        sent = way if sent is None else sent
+        return pltpu.make_async_remote_copy(xs.at[FAR, 1, :, some], rf.at[:, some], f_send, f_recv.at[i], **to(ahead))
+
+    def far_sums():
+        return pltpu.make_async_remote_copy(xs.at[FAR, 1], rf, f_send, f_recv.at[0], **to(ahead))
+
+    def last_sum(i, owner):
         some = pl.ds(sum(LAST_PARTS[:i]) * NT, LAST_PARTS[i] * NT)
-        return pltpu.make_async_remote_copy(
-            xs.at[LAST, 1, block(owner), some], xs.at[OWN, 1 - owner, block(sent), some],
-            l_send.at[i, owner], l_recv.at[i, sent], **to(ahead - core + owner),
-        )
+        src, dst = xs.at[LAST, 1, block(owner), some], xs.at[OWN, 1 - owner, block(way), some]
+        return pltpu.make_async_remote_copy(src, dst, l_send, l_recv.at[i], **to(ahead - core + owner))
+
+    def last_sums(i=None):
+        some = pl.ds(0, depth) if i is None else pl.ds(sum(LAST_PARTS[:i]) * NT, LAST_PARTS[i] * NT)
+        src, dst = xs.at[LAST, 1, :, some], xs.at[OWN, other, :, some]
+        return pltpu.make_async_remote_copy(src, dst, l_send, l_recv.at[i or 0], **to(ahead))
 
     def at_start(parts, t, act):
         for i in range(len(parts)):
@@ -95,10 +113,13 @@
 
     def load_w(j, which):
         src = (wg, wu)[which].at[:, pl.ds(pl.multiple_of(j * FT, FT), FT)]
-        return pltpu.make_async_copy(src, wgu.at[j, :, pl.ds(which * FT, FT)], w_sem.at[which, j])
-
-    def load_wd(t):
-        return pltpu.make_async_copy(wd.at[:, cols(t)], wds.at[t], wd_sem.at[t])
+        return pltpu.make_async_copy(src, wgu.at[j, :, pl.ds(which * FT, FT)], w_sem.at[j])
+
+    def loaded_w(j):
+        return pltpu.make_async_copy(wg.at[:, pl.ds(0, 2 * FT)], wgu.at[j], w_sem.at[j])
+
+    def load_wd():
+        return pltpu.make_async_copy(wd, wds, wd_sem)
 
     def up_stage(stage):
         @pl.loop(0, n_ft * 2)
@@ -108,24 +129,23 @@
 
                 @pl.when(m == 0)
                 def _():
-                    load_w(j, 0).wait()
-                    load_w(j, 1).wait()
+                    loaded_w(j).wait()
 
             both = jnp.dot(xs[stage, m], wgu[j], preferred_element_type=jnp.float32)
             value = (jax.nn.gelu(both[:, :FT]) * both[:, FT:]).astype(jnp.bfloat16)
             h[stage, m, :, pl.ds(pl.multiple_of(j * FT, FT), FT)] = value
 
     def term(stage, which, t):
-        return jnp.dot(h[stage, which], wds[t], preferred_element_type=jnp.float32)
+        return jnp.dot(h[stage, which], wds[:, cols(t)], preferred_element_type=jnp.float32)
 
     def down_for_partner(stage, which, src, slot):
         @pl.loop(0, n_nt)
         def _(t):
             src[:, cols(t)] = term(stage, which, t).astype(jnp.bfloat16)
-            trade(slot, src, t).start()
+            at_end(TRADE_PARTS, t, lambda i: trade(slot, src, i).start())
 
     def chip_sum(stage, which, slot, t):
-        trade(slot, spare, t).wait_recv()
+        at_start(TRADE_PARTS, t, lambda i: trade(slot, spare, i).wait_recv())
         return term(stage, which, t) + rp[slot, :, cols(t)].astype(jnp.float32)
 
     spare = xs.at[NEAR, core]
@@ -154,9 +174,7 @@
         load_w(j, 0).start()
         load_w(j, 1).start()
 
-    @pl.loop(0, n_nt)
-    def _(t):
-        load_wd(t).start()
+    load_wd().start()
 
     @pl.when(core == 1)
     def _():
@@ -164,8 +182,7 @@
 
     for i in range(2):
         share(OWN, i).start()
-    share(OWN, 0).wait_recv()
-    share(OWN, 1).wait_recv()
+    shared(OWN).wait_recv()
     gather(NEAR, 1).start()
     load_x().wait()
     up_stage(OWN)
@@ -176,15 +193,12 @@
         share(NEAR, i).start()
     for i in range(2):
         gather(LAST, i).start()
-    for i in range(2):
-        share(NEAR, i).wait_recv()
+    shared(NEAR).wait_recv()
     for writer in (behind, beside):
         pl.semaphore_signal(credit, inc=1, **to(writer))
     up_stage(NEAR)
 
-    @pl.loop(0, n_nt)
-    def _(t):
-        load_wd(t).wait()
+    load_wd().wait()
 
     down_for_partner(NEAR, other, spare, 0)
 
@@ -199,8 +213,7 @@
     for i in range(2):
         gather(FAR, i).wait_recv()
         share(FAR, i).start()
-    for i in range(2):
-        share(FAR, i).wait()
+    shared(FAR).wait()
     up_stage(FAR)
     down_for_partner(FAR, core, xs.at[FAR, 0], 1)
 
@@ -212,19 +225,15 @@
     for i in range(2):
         gather(LAST, i).wait_recv()
         share(LAST, i).start()
-    for i in range(2):
-        gather(LAST, i).wait_send()
-        gather(NEAR, i).wait_send()
+    gathered(LAST).wait_send()
+    gathered(NEAR).wait_send()
     for writer in (behind, beside):
         pl.semaphore_signal(late_credit, inc=1, **to(writer))
-    for i in range(2):
-        share(LAST, i).wait()
+    shared(LAST).wait()
     up_stage(LAST)
 
-    @pl.loop(0, n_nt)
-    def _(t):
-        trade(0, spare, t).wait_send()
-        trade(1, xs.at[FAR, 0], t).wait_send()
+    traded(0, spare).wait_send()
+    traded(1, xs.at[FAR, 0]).wait_send()
 
     down_for_partner(LAST, other, xs.at[LAST, 0], 0)
     down_for_partner(OWN, other, spare, 1)
@@ -242,35 +251,24 @@
         xs[LAST, 1, :, cols(t)] = total.astype(jnp.bfloat16)
         at_end(LAST_PARTS, t, send_last)
 
-    for sent in range(2):
-        near_sum(core, sent).wait_recv()
-
-    def await_last(i):
-        for sent in range(2):
-            last_sum(i, core, sent).wait_recv()
+    near_sums().wait_recv()
+
+    traded(0, xs.at[LAST, 0]).wait_send()
+    traded(1, spare).wait_send()
+    gathered(FAR).wait_send()
+    shared(OWN).wait_send()
+    shared(NEAR).wait_send()
+    near_sums().wait_send()
+    far_sums().wait_send()
 
     @pl.loop(0, n_nt)
     def _(t):
         total = chip_sum(OWN, core, 1, t) + xs[OWN, core, :, cols(t)].astype(jnp.float32)
-        at_start(LAST_PARTS, t, await_last)
+        at_start(LAST_PARTS, t, lambda i: last_sums(i).wait_recv())
         total = total + xs[OWN, other, :, cols(t)].astype(jnp.float32)
         y[:, cols(t)] = total.astype(jnp.bfloat16)
 
-    @pl.loop(0, n_nt)
-    def _(t):
-        trade(0, xs.at[LAST, 0], t).wait_send()
-        trade(1, spare, t).wait_send()
-
-    for i in range(2):
-        gather(FAR, i).wait_send()
-        share(OWN, i).wait_send()
-        share(NEAR, i).wait_send()
-        near_sum(i).wait_send()
-    for i in range(len(FAR_PARTS)):
-        far_sum(i).wait_send()
-    for i in range(len(LAST_PARTS)):
-        for owner in range(2):
-            last_sum(i, owner).wait_send()
+    last_sums().wait_send()
 
 
 def solution(mesh):
@@ -290,25 +288,25 @@
             scratch_shapes=[
                 pltpu.VMEM((4, 2, rows, depth), jnp.bfloat16),
                 pltpu.VMEM((n_ft, depth, 2 * FT), jnp.bfloat16),
-                pltpu.VMEM((n_nt, hidden, NT), jnp.bfloat16),
+                pltpu.VMEM((hidden, depth), jnp.bfloat16),
                 pltpu.VMEM((4, 2, rows, hidden), jnp.bfloat16),
                 pltpu.VMEM((2, rows, depth), jnp.bfloat16),
                 pltpu.VMEM((rows, depth), jnp.bfloat16),
                 pltpu.VMEM((rows, depth), jnp.bfloat16),
-                dma((4, 2)),
-                dma((4, 2)),
-                dma((4, 2)),
-                dma((4, 2)),
-                dma((2, n_nt)),
-                dma((2, n_nt)),
+                dma((3,)),
+                dma((3, 2)),
+                dma((4,)),
+                dma((4,)),
                 dma((2,)),
-                dma((2,)),
+                dma((2, len(TRADE_PARTS))),
+                dma,
+                dma,
+                dma,
                 dma((len(FAR_PARTS),)),
-                dma((len(FAR_PARTS),)),
-                dma((len(LAST_PARTS), 2)),
-                dma((len(LAST_PARTS), 2)),
-                dma((2, n_ft)),
-                dma((n_nt,)),
+                dma,
+                dma((len(LAST_PARTS),)),
+                dma((n_ft,)),
+                dma,
                 dma,
                 plain,
                 plain,

time: 142 us -> 142 us (level)
  no operation moved by 1% of the time
where the time goes in v5:
time: 142 us; the launch traced here: 141 us
  Pallas kernels  140 us (99%)
    pallas_call x1, Pallas kernels, step(): pl.pallas_call(functools.partial(kernel, n), out_shape=pltpu.VMEM((rows,...  140 us

profile of v5, /device:TPU:112, one launch (start us, length us, event | category | flops | bytes accessed | tf_op | source)
XLA Modules:
  0.0 141.5 jit_solution(494942557742487298)
XLA Ops:
  0.0 140.2 %shard_map.46 = bf16[256,4096]{1,0:T(8,128)(2,1)S(1)} custom-call(bf16[256,4096]{1,0:T(8,128)(2,1)} %x.1, bf16[4096,1280]{1,0:T(8,128)(2,1)} %wg.1, bf16[4096,1280]{1,0:T(8,128)(2,1)} %wu.1, bf16[1280,4096]{1,0:T(8,128)(2,1)} %wd.1), custom_call_target="tpu_custom_call" | custom-call | flops 64424509440 | bytes 31457280 | tf_op jit(solution)/shard_map/pallas_call | solution.py:283
  140.2 1.3 copy.6

commit v6 on v5

--- a/solution.py
+++ b/solution.py
@@ -11,14 +11,14 @@
 FT = 256
 NT = 512
 FAR_PARTS = (4, 4)
-TRADE_PARTS = (4, 4)
+TRADE_PARTS = (8,)
 LAST_PARTS = (4, 3, 1)
 OWN, NEAR, FAR, LAST = range(4)
 
 
 def kernel(
     n, x, wg, wu, wd, y, xs, wgu, wds, h, rp, rf, stg,
-    g_send, g_recv, d_send, d_recv, p_send, p_recv, n_send, n_recv, f_send, f_recv, l_send, l_recv,
+    g_send, g_recv, d_send, d_recv, p_send, p_recv, s_send, n_recv, f_recv, l_recv,
     w_sem, wd_sem, x_sem, ready, credit, late_credit,
 ):
     rows, depth = x.shape
@@ -49,11 +49,15 @@
         part = block(1 - way if stage == LAST else way)
         src = xs.at[NEAR, way, block(origin)] if stage == FAR else (x.at[part], xs.at[OWN, other, part])[i]
         dst = xs.at[stage, way, block(origin)]
-        return pltpu.make_async_remote_copy(src, dst, g_send.at[stage - 1], g_recv.at[stage - 1, i], **to(ahead))
+        return pltpu.make_async_remote_copy(src, dst, g_send, g_recv.at[i if stage == NEAR else stage], **to(ahead))
 
     def gathered(stage):
         both = xs.at[stage, way]
-        return pltpu.make_async_remote_copy(both, both, g_send.at[stage - 1], g_recv.at[stage - 1, 0], **to(ahead))
+        return pltpu.make_async_remote_copy(both, both, g_send, g_recv.at[stage], **to(ahead))
+
+    def all_out(sem):
+        three = xs.at[pl.ds(NEAR, 3), 0]
+        return pltpu.make_async_remote_copy(three, three, sem, g_recv.at[0], **to(ahead))
 
     def share(stage, i):
         if stage == OWN:
@@ -61,11 +65,11 @@
             src, dst = x.at[part], xs.at[OWN, core, part]
         else:
             src = dst = xs.at[stage, way, block((core, other)[i])]
-        return pltpu.make_async_remote_copy(src, dst, d_send.at[stage], d_recv.at[stage], **to(partner))
+        return pltpu.make_async_remote_copy(src, dst, d_send.at[stage % 2], d_recv.at[stage % 2], **to(partner))
 
     def shared(stage):
         src, dst = (x, xs.at[OWN, core]) if stage == OWN else (xs.at[stage, way],) * 2
-        return pltpu.make_async_remote_copy(src, dst, d_send.at[stage], d_recv.at[stage], **to(partner))
+        return pltpu.make_async_remote_copy(src, dst, d_send.at[stage % 2], d_recv.at[stage % 2], **to(partner))
 
     def trade(slot, src, i):
         some = pl.ds(sum(TRADE_PARTS[:i]) * NT, TRADE_PARTS[i] * NT)
@@ -78,27 +82,24 @@
 
     def near_sum(owner):
         dst = xs.at[OWN, owner, block(1 - way)]
-        return pltpu.make_async_remote_copy(stg.at[block(owner)], dst, n_send, n_recv, **to(ahead - core + owner))
+        return pltpu.make_async_remote_copy(stg.at[block(owner)], dst, s_send, n_recv, **to(ahead - core + owner))
 
     def near_sums():
-        return pltpu.make_async_remote_copy(stg, xs.at[OWN, core], n_send, n_recv, **to(ahead))
+        return pltpu.make_async_remote_copy(stg, xs.at[OWN, core], s_send, n_recv, **to(ahead))
 
     def far_sum(i):
         some = pl.ds(sum(FAR_PARTS[:i]) * NT, FAR_PARTS[i] * NT)
-        return pltpu.make_async_remote_copy(xs.at[FAR, 1, :, some], rf.at[:, some], f_send, f_recv.at[i], **to(ahead))
-
-    def far_sums():
-        return pltpu.make_async_remote_copy(xs.at[FAR, 1], rf, f_send, f_recv.at[0], **to(ahead))
+        return pltpu.make_async_remote_copy(xs.at[FAR, 1, :, some], rf.at[:, some], s_send, f_recv.at[i], **to(ahead))
 
     def last_sum(i, owner):
         some = pl.ds(sum(LAST_PARTS[:i]) * NT, LAST_PARTS[i] * NT)
         src, dst = xs.at[LAST, 1, block(owner), some], xs.at[OWN, 1 - owner, block(way), some]
-        return pltpu.make_async_remote_copy(src, dst, l_send, l_recv.at[i], **to(ahead - core + owner))
-
-    def last_sums(i=None):
-        some = pl.ds(0, depth) if i is None else pl.ds(sum(LAST_PARTS[:i]) * NT, LAST_PARTS[i] * NT)
+        return pltpu.make_async_remote_copy(src, dst, s_send, l_recv.at[i], **to(ahead - core + owner))
+
+    def last_sums(i):
+        some = pl.ds(sum(LAST_PARTS[:i]) * NT, LAST_PARTS[i] * NT)
         src, dst = xs.at[LAST, 1, :, some], xs.at[OWN, other, :, some]
-        return pltpu.make_async_remote_copy(src, dst, l_send, l_recv.at[i or 0], **to(ahead))
+        return pltpu.make_async_remote_copy(src, dst, s_send, l_recv.at[i], **to(ahead))
 
     def at_start(parts, t, act):
         for i in range(len(parts)):
@@ -210,9 +211,9 @@
     for owner in range(2):
         near_sum(owner).start()
 
-    for i in range(2):
-        gather(FAR, i).wait_recv()
-        share(FAR, i).start()
+    gathered(FAR).wait_recv()
+    shared(OWN).wait_send()
+    shared(FAR).start()
     shared(FAR).wait()
     up_stage(FAR)
     down_for_partner(FAR, core, xs.at[FAR, 0], 1)
@@ -222,11 +223,10 @@
         xs[FAR, 1, :, cols(t)] = chip_sum(FAR, other, 1, t).astype(jnp.bfloat16)
         at_end(FAR_PARTS, t, lambda i: far_sum(i).start())
 
-    for i in range(2):
-        gather(LAST, i).wait_recv()
-        share(LAST, i).start()
-    gathered(LAST).wait_send()
-    gathered(NEAR).wait_send()
+    gathered(LAST).wait_recv()
+    shared(NEAR).wait_send()
+    shared(LAST).start()
+    all_out(g_send).wait_send()
     for writer in (behind, beside):
         pl.semaphore_signal(late_credit, inc=1, **to(writer))
     shared(LAST).wait()
@@ -255,11 +255,6 @@
 
     traded(0, xs.at[LAST, 0]).wait_send()
     traded(1, spare).wait_send()
-    gathered(FAR).wait_send()
-    shared(OWN).wait_send()
-    shared(NEAR).wait_send()
-    near_sums().wait_send()
-    far_sums().wait_send()
 
     @pl.loop(0, n_nt)
     def _(t):
@@ -268,7 +263,7 @@
         total = total + xs[OWN, other, :, cols(t)].astype(jnp.float32)
         y[:, cols(t)] = total.astype(jnp.bfloat16)
 
-    last_sums().wait_send()
+    all_out(s_send).wait_send()
 
 
 def solution(mesh):
@@ -293,17 +288,15 @@
                 pltpu.VMEM((2, rows, depth), jnp.bfloat16),
                 pltpu.VMEM((rows, depth), jnp.bfloat16),
                 pltpu.VMEM((rows, depth), jnp.bfloat16),
-                dma((3,)),
-                dma((3, 2)),
-                dma((4,)),
+                dma,
                 dma((4,)),
                 dma((2,)),
+                dma((2,)),
+                dma((2,)),
                 dma((2, len(TRADE_PARTS))),
                 dma,
                 dma,
-                dma,
                 dma((len(FAR_PARTS),)),
-                dma,
                 dma((len(LAST_PARTS),)),
                 dma((n_ft,)),
                 dma,

time: 142 us -> 141 us (level)
  no operation moved by 1% of the time
where the time goes in v6:
time: 141 us
  Pallas kernels  140 us (99%)
    pallas_call x1, Pallas kernels, step(): pl.pallas_call(functools.partial(kernel, n), out_shape=pltpu.VMEM((rows,...  140 us

profile of v6, /device:TPU:112, one launch (start us, length us, event | category | flops | bytes accessed | tf_op | source)
XLA Modules:
  0.0 141.4 jit_solution(691261051746537297)
XLA Ops:
  0.0 140.0 %shard_map.46 = bf16[256,4096]{1,0:T(8,128)(2,1)S(1)} custom-call(bf16[256,4096]{1,0:T(8,128)(2,1)} %x.1, bf16[4096,1280]{1,0:T(8,128)(2,1)} %wg.1, bf16[4096,1280]{1,0:T(8,128)(2,1)} %wu.1, bf16[1280,4096]{1,0:T(8,128)(2,1)} %wd.1), custom_call_target="tpu_custom_call" | custom-call | flops 64424509440 | bytes 31457280 | tf_op jit(solution)/shard_map/pallas_call | solution.py:278
  140.1 1.3 copy.6

commit v7 on v6

--- a/solution.py
+++ b/solution.py
@@ -19,7 +19,7 @@
 def kernel(
     n, x, wg, wu, wd, y, xs, wgu, wds, h, rp, rf, stg,
     g_send, g_recv, d_send, d_recv, p_send, p_recv, s_send, n_recv, f_recv, l_recv,
-    w_sem, wd_sem, x_sem, ready, credit, late_credit,
+    w_sem, wd_sem, ready, credit, late_credit,
 ):
     rows, depth = x.shape
     hidden = wg.shape[1]
@@ -110,7 +110,11 @@
             pl.when(t == sum(parts[: i + 1]) - 1)(functools.partial(act, i))
 
     def load_x():
-        return pltpu.make_async_copy(x, xs.at[OWN, core], x_sem)
+        return pltpu.make_async_copy(x, xs.at[OWN, core], d_recv.at[OWN])
+
+    def own_rows():
+        both = xs.at[OWN]
+        return pltpu.make_async_remote_copy(both, both, d_send.at[OWN], d_recv.at[OWN], **to(partner))
 
     def load_w(j, which):
         src = (wg, wu)[which].at[:, pl.ds(pl.multiple_of(j * FT, FT), FT)]
@@ -183,9 +187,8 @@
 
     for i in range(2):
         share(OWN, i).start()
-    shared(OWN).wait_recv()
+    own_rows().wait_recv()
     gather(NEAR, 1).start()
-    load_x().wait()
     up_stage(OWN)
 
     for i in range(2):
@@ -300,7 +303,6 @@
                 dma((len(LAST_PARTS),)),
                 dma((n_ft,)),
                 dma,
-                dma,
                 plain,
                 plain,
                 plain,

time: 141 us -> 141 us (level)
  no operation moved by 1% of the time
where the time goes in v7:
time: 141 us
  Pallas kernels  140 us (99%)
    pallas_call x1, Pallas kernels, step(): pl.pallas_call(functools.partial(kernel, n), out_shape=pltpu.VMEM((rows,...  140 us

profile of v7, /device:TPU:112, one launch (start us, length us, event | category | flops | bytes accessed | tf_op | source)
XLA Modules:
  0.0 141.4 jit_solution(8019470604035445846)
XLA Ops:
  0.0 140.0 %shard_map.46 = bf16[256,4096]{1,0:T(8,128)(2,1)S(1)} custom-call(bf16[256,4096]{1,0:T(8,128)(2,1)} %x.1, bf16[4096,1280]{1,0:T(8,128)(2,1)} %wg.1, bf16[4096,1280]{1,0:T(8,128)(2,1)} %wu.1, bf16[1280,4096]{1,0:T(8,128)(2,1)} %wd.1), custom_call_target="tpu_custom_call" | custom-call | flops 64424509440 | bytes 31457280 | tf_op jit(solution)/shard_map/pallas_call | solution.py:281
  140.0 1.3 copy.6
